TPU v7x, 32 devices: a whole 2x2x4 slice. The times are simulated.
32 devices in a mesh: grp: 4 (over y, x), slab: 8 (over z, core).
Axes of the slice: x: 2, y: 2, z: 4, core: 2. Of those that a mesh axis runs over, the one named last changes fastest.
Arguments:
- state: float32 [4, 2, 256, 128, 256], P(None, None, 'grp', 'slab'), may hold values from -5.6 to 5.6
- kz_group: int32 [256], replicated, may hold values from 0 to 7, as said below
- cutoffs: int32 [3], replicated, may hold values from 28 to 32
- damping: float32 [8], replicated, may hold values from 0.005 to 0.5
- power: float32 [8], replicated, may hold values from 0.2 to 4
Outputs:
- new_state: float32 [4, 2, 256, 128, 256], P(None, None, 'grp', 'slab')
Inputs may be any that keep to these rules, and one draw needn't show every extreme that they name: `kz_group`: each of the 8 groups holds exactly 32 indices.
All inputs are finite; a program needn't handle non-finite values.
Results may differ from a plain program's by a relative error of at most 0.00005.
Values sent between devices are 32-bit elements; how exact they have to be, the bound alone decides.
A program may use at most 192 MiB of HBM per device.

v0:
```python
import math

import jax
import jax.numpy as jnp
from jax import lax
from jax.sharding import PartitionSpec as P

NX = 256
NY = 256
NZ = 256
GROUPS = 8
KX = 128
GMODES = 32


PRECISE = lax.Precision.HIGHEST
TWO_PI = 6.283185307179586
TIME_STEP = 0.25
CORIOLIS = 1.0
BRUNT_SQUARED = 2.0
EPSILON = 1e-06


def signed(index, length):
    return jnp.where(index < length // 2, index, index - length)


def angles(modes, points, length):
    phase = modes[:, None] * points[None, :] % length
    theta = phase.astype(jnp.float32) * (TWO_PI / length)
    return (jnp.cos(theta), jnp.sin(theta))


def rotate(pattern, real_part, imag_part, cosine_table, sine_table, forward):
    first = jnp.einsum(pattern, real_part, cosine_table, precision=PRECISE)
    second = jnp.einsum(pattern, imag_part, sine_table, precision=PRECISE)
    third = jnp.einsum(pattern, real_part, sine_table, precision=PRECISE)
    fourth = jnp.einsum(pattern, imag_part, cosine_table, precision=PRECISE)
    if forward:
        return (first + second, fourth - third)
    return (first - second, third + fourth)


def times_i(entries):
    return jnp.stack([-entries[1], entries[0]])


def x_forward(products, pattern, cosine_table, sine_table):
    real_x = jnp.einsum(pattern, products, cosine_table, precision=PRECISE)
    imag_x = -jnp.einsum(pattern, products, sine_table, precision=PRECISE)
    return (real_x, imag_x)


def shards(state, kz_group, cutoffs, damping, power):
    grp_count = lax.axis_size("grp")
    grp_index = lax.axis_index("grp")
    slab_index = lax.axis_index("slab")
    slots_here = state.shape[2]
    cols_here = state.shape[3]
    groups_here = GROUPS // grp_count
    normalizer = 1.0 / math.sqrt(NX * NY * NZ)
    slot_mode = jnp.argsort(kz_group, stable=True)
    local_mode = lax.dynamic_slice_in_dim(slot_mode, grp_index * slots_here, slots_here)
    mode_z = signed(local_mode, NZ)
    mode_x = slab_index * cols_here + jnp.arange(cols_here, dtype=jnp.int32)
    mode_y = signed(jnp.arange(NY, dtype=jnp.int32), NY)
    wave_z = (TWO_PI / NZ * mode_z.astype(jnp.float32))[:, None, None]
    wave_x = (TWO_PI / NX * mode_x.astype(jnp.float32))[None, :, None]
    wave_y = (TWO_PI / NY * mode_y.astype(jnp.float32))[None, None, :]
    flow_x, flow_y, flow_z, buoyant = (state[0], state[1], state[2], state[3])
    means = None
    swirl_x = times_i(wave_y * flow_z - wave_z * flow_y)
    swirl_y = times_i(wave_z * flow_x - wave_x * flow_z)
    swirl_z = times_i(wave_x * flow_y - wave_y * flow_x)
    fields = jnp.stack([flow_x, flow_y, flow_z, buoyant, swirl_x, swirl_y, swirl_z])
    cosine_y, sine_y = angles(jnp.arange(NY, dtype=jnp.int32), jnp.arange(NY, dtype=jnp.int32), NY)
    real_y, imag_y = rotate("fzxm,my->fzxy", fields[:, 0], fields[:, 1], cosine_y, sine_y, False)
    spectral_y = jnp.stack([real_y, imag_y], axis=1)
    cosine_zi, sine_zi = angles(slot_mode, jnp.arange(NZ, dtype=jnp.int32), NZ)
    cosine_zf, sine_zf = angles(jnp.arange(NZ, dtype=jnp.int32), slot_mode, NZ)
    weights = jnp.where(jnp.arange(KX) == 0, 1.0, 2.0).astype(jnp.float32) * normalizer
    cosine_x, sine_x = angles(jnp.arange(KX, dtype=jnp.int32), jnp.arange(NX, dtype=jnp.int32), NX)
    cosine_x = cosine_x * weights[:, None]
    sine_x = sine_x * weights[:, None]
    cosine_xf, sine_xf = angles(
        jnp.arange(NX, dtype=jnp.int32), jnp.arange(KX, dtype=jnp.int32), NX
    )
    pieces = lax.all_to_all(spectral_y, "grp", split_axis=4, concat_axis=2, tiled=True)
    real_part, imag_part = rotate(
        "fsxy,sz->fzxy", pieces[:, 0], pieces[:, 1], cosine_zi, sine_zi, False
    )
    grid_z = jnp.stack([real_part, imag_part], axis=1)
    pieces = lax.all_to_all(grid_z, "slab", split_axis=2, concat_axis=3, tiled=True)
    physical = jnp.einsum("fzky,kn->fzyn", pieces[:, 0], cosine_x, precision=PRECISE) - jnp.einsum(
        "fzky,kn->fzyn", pieces[:, 1], sine_x, precision=PRECISE
    )
    grid_u = physical[0]
    grid_v = physical[1]
    grid_w = physical[2]
    grid_b = physical[3]
    grid_ox = physical[4]
    grid_oy = physical[5]
    grid_oz = physical[6]
    products = jnp.stack(
        [
            grid_v * grid_oz - grid_w * grid_oy,
            grid_w * grid_ox - grid_u * grid_oz,
            grid_u * grid_oy - grid_v * grid_ox,
            grid_u * grid_b,
            grid_v * grid_b,
            grid_w * grid_b,
        ]
    )
    real_x, imag_x = x_forward(products, "fzyn,nk->fzky", cosine_xf, sine_xf)
    sectioned = jnp.stack([real_x, imag_x], axis=1)
    pieces = lax.all_to_all(sectioned, "slab", split_axis=3, concat_axis=2, tiled=True)
    real_part, imag_part = rotate(
        "fzxy,zs->fsxy", pieces[:, 0], pieces[:, 1], cosine_zf, sine_zf, True
    )
    spectral_z = jnp.stack([real_part, imag_part], axis=1)
    pieces = lax.all_to_all(spectral_z, "grp", split_axis=2, concat_axis=4, tiled=True)
    real_part, imag_part = rotate(
        "fsxy,ym->fsxm", pieces[:, 0], pieces[:, 1], cosine_y, sine_y, True
    )
    tendency = jnp.stack([real_part, imag_part], axis=1) * normalizer
    real_part = state[:, 0]
    imag_part = state[:, 1]
    cell_flux = real_part[2] * real_part[3] + imag_part[2] * imag_part[3]
    cell_energy = 0.5 * (
        jnp.sum(real_part[:3] ** 2 + imag_part[:3] ** 2, axis=0)
        + (real_part[3] ** 2 + imag_part[3] ** 2) / BRUNT_SQUARED
    )
    partial_value = jnp.stack(
        [jnp.sum(cell_flux, axis=(1, 2)), jnp.sum(cell_energy, axis=(1, 2))], axis=1
    )
    partial_value = jnp.sum(partial_value.reshape(groups_here, GMODES, 2), axis=1)
    totals = lax.psum(partial_value, "slab")
    means = totals / (GMODES * KX * NY)
    kept = (
        (96 * jnp.abs(mode_z) <= cutoffs[2] * NZ)[:, None, None]
        & (96 * mode_x <= cutoffs[0] * NX)[None, :, None]
        & (96 * jnp.abs(mode_y) <= cutoffs[1] * NY)[None, None, :]
    ).astype(jnp.float32)
    moment_x, moment_y, moment_z = (tendency[0] * kept, tendency[1] * kept, tendency[2] * kept)
    divergence = wave_x * tendency[3] + wave_y * tendency[4] + wave_z * tendency[5]
    source_b = jnp.stack([divergence[1], -divergence[0]]) * kept
    power_here = lax.dynamic_slice_in_dim(power, grp_index * groups_here, groups_here)
    damping_here = lax.dynamic_slice_in_dim(damping, grp_index * groups_here, groups_here)
    forcing = (power_here - means[:, 0]) / (2.0 * (means[:, 1] + EPSILON))
    forcing_slot = jnp.repeat(forcing, GMODES)[:, None, None]
    damping_slot = jnp.repeat(damping_here, GMODES)[:, None, None]
    right_x = flow_x + TIME_STEP * (moment_x + forcing_slot * flow_x)
    right_y = flow_y + TIME_STEP * (moment_y + forcing_slot * flow_y)
    right_z = flow_z + TIME_STEP * (moment_z + forcing_slot * flow_z)
    right_b = buoyant + TIME_STEP * source_b
    wave_sq = wave_x * wave_x + wave_y * wave_y + wave_z * wave_z
    implicit = 1.0 + TIME_STEP * damping_slot * wave_sq
    rotation = TIME_STEP * CORIOLIS
    first_den = implicit * implicit + rotation * rotation
    second_den = implicit * implicit + TIME_STEP * TIME_STEP * BRUNT_SQUARED
    new_x = (implicit * right_x + rotation * right_y) / first_den
    new_y = (implicit * right_y - rotation * right_x) / first_den
    new_z = (implicit * right_z + TIME_STEP * right_b) / second_den
    new_b = (implicit * right_b - TIME_STEP * BRUNT_SQUARED * right_z) / second_den
    inverse_sq = 1.0 / (wave_sq + (wave_sq == 0).astype(jnp.float32))
    inner = (wave_x * new_x + wave_y * new_y + wave_z * new_z) * inverse_sq
    new_x = new_x - wave_x * inner
    new_y = new_y - wave_y * inner
    new_z = new_z - wave_z * inner
    return jnp.stack([new_x, new_y, new_z, new_b])


def solution(mesh):
    return jax.shard_map(
        shards,
        mesh=mesh,
        in_specs=(P(None, None, "grp", "slab", None), P(), P(), P(), P()),
        out_specs=P(None, None, "grp", "slab", None),
        check_vma=False,
    )
```

profile of v0, /device:TPU:0, one launch (start us, length us, event | category | flops | bytes accessed | tf_op | source)
XLA Modules:
  0.0 2021.2 jit_solution(9663195333022750134)
XLA Ops:
  63.3 27.2 %copy.46 = f32[7,2,64,16,256]{2,3,1,0,4:T(8,128)} copy(f32[7,2,64,16,256]{4,3,2,0,1:T(8,128)} %pad_maximum_fusion.1) | data formatting | bytes 29360128 | tf_op jit(solution)/shard_map/stack | solution.py:78
  90.5 37.7 %reshape.239 = f32[4,1,917504]{2,1,0:T(1,128)} reshape(f32[256,7,2,16,64]{4,3,2,1,0:T(8,128)} %bitcast.261) | data formatting | bytes 29360128
  128.2 172.1 %all_to_all.72 = f32[4,1,917504]{2,1,0:T(1,128)} all-to-all(f32[4,1,917504]{2,1,0:T(1,128)} %reshape.239), channel_id=1, replica_groups=mesh['grp'=4,'slab'=8] {'grp'}, dimensions={0} | all-to-all | bytes 29360128 | tf_op jit(solution)/shard_map/all_to_all | solution.py:88
  300.8 46.1 %reduce.2 = f32[4,917504]{1,0:T(4,128)} reduce(f32[4,1,917504]{2,1,0:T(1,128)} %all_to_all.72, f32[]{:T(128)} %broadcast.529), dimensions={1}, to_apply=%all_to_all.52.reduce_sub_computation | reduce | bytes 29360132 | tf_op jit(solution)/shard_map/all_to_all | solution.py:88
  346.9 42.0 %reshape.240 = f32[256,7,2,16,64]{4,3,2,1,0:T(8,128)} reshape(f32[4,917504]{1,0:T(4,128)} %reduce.2) | data formatting | bytes 29360128
  388.9 33.7 %copy.76 = f32[7,2,64,16,4,64]{2,4,5,3,0,1:T(4,128)} copy(f32[7,2,64,16,4,64]{2,3,1,0,5,4:T(8,128)} %bitcast.258) | data formatting | bytes 29360128 | tf_op jit(solution)/shard_map/all_to_all | solution.py:88
  422.6 26.9 %all_to_all.55 = f32[7,2,256,16,64]{2,4,3,0,1:T(8,128)} reshape(f32[7,2,4,64,16,64]{3,2,5,4,0,1:T(4,128)} %bitcast.259) | data formatting | bytes 29360128 | tf_op jit(solution)/shard_map/all_to_all | solution.py:88
  449.5 13.3 fusion.204
  522.1 13.1 pad_maximum_fusion.2
  535.2 27.2 %copy.48 = f32[7,2,256,16,64]{4,3,0,1,2:T(8,128)} copy(f32[7,2,256,16,64]{2,4,3,0,1:T(8,128)} %pad_maximum_fusion.2) | data formatting | bytes 29360128 | tf_op jit(solution)/shard_map/stack | solution.py:92
  562.4 23.1 %reshape.241 = f32[8,1,458752]{2,1,0:T(1,128)} reshape(f32[256,2,7,16,64]{4,3,2,1,0:T(8,128)} %bitcast.262) | data formatting | bytes 29360128
  591.1 318.7 %all-to-all-done.1 = f32[8,1,458752]{2,1,0:T(1,128)} async-done(((f32[8,1,458752]{2,1,0:T(1,128)}), f32[8,1,458752]{2,1,0:T(1,128)}, u32[]{:S(2)}, u32[]{:S(2)}) %all-to-all-start.1) | async-done | bytes 14680096 | tf_op jit(solution)/shard_map/all_to_all | solution.py:93
  909.7 42.5 %reduce.3 = f32[8,458752]{1,0:T(8,128)} reduce(f32[8,1,458752]{2,1,0:T(1,128)} %all-to-all-done.1, f32[]{:T(128)} %broadcast.529), dimensions={1}, to_apply=%all_to_all.56.reduce_sub_computation | reduce | bytes 29360132 | tf_op jit(solution)/shard_map/all_to_all | solution.py:93
  952.2 26.2 %reshape.242 = f32[256,2,7,16,64]{4,3,2,1,0:T(8,128)} reshape(f32[8,458752]{1,0:T(8,128)} %reduce.3) | data formatting | bytes 29360128
  978.5 22.4 %copy.50 = f32[7,2,32,8,16,64]{5,4,3,2,1,0:T(8,128)} copy(f32[7,2,32,8,16,64]{5,4,0,1,2,3:T(8,128)} %bitcast.260) | data formatting | bytes 29360128 | tf_op jit(solution)/shard_map/all_to_all | solution.py:93
  1000.9 30.6 %fusion = f32[7,32,64,256]{3,2,1,0:T(8,128)} fusion(f32[7,2,32,128,64]{4,3,2,1,0:T(8,128)} %bitcast.256, f32[128]{0:T(128)S(1)} %fusion.119), kind=kOutput, calls=%fused_computation.3 | convolution fusion | flops 5637636096 | bytes 29360640 | tf_op jit(solution)/shard_map/fzky,kn->fzyn/dot_general | solution.py:94
  1031.5 32.3 %fusion.2 = f32[7,32,64,256]{3,2,1,0:T(8,128)} fusion(f32[7,32,64,256]{3,2,1,0:T(8,128)} %fusion, f32[7,2,32,128,64]{4,3,2,1,0:T(8,128)} %bitcast.257, f32[128]{0:T(128)S(1)} %fusion.119), kind=kOutput, calls=%fused_computation.12 | convolution fusion | flops 5641306112 | bytes 44040704 | tf_op jit(solution)/shard_map/fzky,kn->fzyn/dot_general | solution.py:94
  1109.7 23.4 %copy.53 = f32[6,2,32,128,64]{4,2,0,1,3:T(8,128)} copy(f32[6,2,32,128,64]{3,4,2,0,1:T(8,128)} %pad_maximum_fusion.3) | data formatting | bytes 25165824 | tf_op jit(solution)/shard_map/stack | solution.py:115
  1133.1 20.7 %reshape.243 = f32[8,1,393216]{2,1,0:T(1,128)} reshape(f32[128,2,6,32,64]{4,3,2,1,0:T(8,128)} %bitcast.264) | data formatting | bytes 25165824
  1153.8 280.5 %all_to_all.73 = f32[8,1,393216]{2,1,0:T(1,128)} all-to-all(f32[8,1,393216]{2,1,0:T(1,128)} %reshape.243), channel_id=1, replica_groups=mesh['grp'=4,'slab'=8] {'slab'}, dimensions={0} | all-to-all | bytes 25165824 | tf_op jit(solution)/shard_map/all_to_all | solution.py:116
  1434.2 36.7 %reduce.4 = f32[8,393216]{1,0:T(8,128)} reduce(f32[8,1,393216]{2,1,0:T(1,128)} %all_to_all.73, f32[]{:T(128)} %broadcast.529), dimensions={1}, to_apply=%all_to_all.60.reduce_sub_computation | reduce | bytes 25165828 | tf_op jit(solution)/shard_map/all_to_all | solution.py:116
  1470.9 22.6 %reshape.244 = f32[128,2,6,32,64]{4,3,2,1,0:T(8,128)} reshape(f32[8,393216]{1,0:T(8,128)} %reduce.4) | data formatting | bytes 25165824
  1493.5 28.3 %copy.55 = f32[6,2,8,32,16,64]{5,4,3,2,1,0:T(8,128)} copy(f32[6,2,8,32,16,64]{5,3,0,1,4,2:T(8,128)} %bitcast.265) | data formatting | bytes 25165824 | tf_op jit(solution)/shard_map/all_to_all | solution.py:116
  1521.8 18.0 fusion.203
  1622.2 23.4 %copy.58 = f32[6,2,256,16,64]{4,3,0,1,2:T(8,128)} copy(f32[6,2,256,16,64]{2,4,3,0,1:T(8,128)} %pad_maximum_fusion.4) | data formatting | bytes 25165824 | tf_op jit(solution)/shard_map/stack | solution.py:120
  1645.6 33.5 %reshape.245 = f32[4,1,786432]{2,1,0:T(1,128)} reshape(f32[256,2,6,16,64]{4,3,2,1,0:T(8,128)} %bitcast.266) | data formatting | bytes 25165824
  1694.4 14.5 psum.7
  1715.6 107.0 %all-to-all-done.3 = f32[4,1,786432]{2,1,0:T(1,128)} async-done(((f32[4,1,786432]{2,1,0:T(1,128)}), f32[4,1,786432]{2,1,0:T(1,128)}, u32[]{:S(2)}, u32[]{:S(2)}) %all-to-all-start.3) | async-done | bytes 12582944 | tf_op jit(solution)/shard_map/all_to_all | solution.py:121
  1822.6 40.1 %reduce.5 = f32[4,786432]{1,0:T(4,128)} reduce(f32[4,1,786432]{2,1,0:T(1,128)} %all-to-all-done.3, f32[]{:T(128)} %broadcast.529), dimensions={1}, to_apply=%all_to_all.64.reduce_sub_computation | reduce | bytes 25165828 | tf_op jit(solution)/shard_map/all_to_all | solution.py:121
  1862.7 31.9 %reshape.246 = f32[256,2,6,16,64]{4,3,2,1,0:T(8,128)} reshape(f32[4,786432]{1,0:T(4,128)} %reduce.5) | data formatting | bytes 25165824
  1894.6 30.2 %copy.77 = f32[6,2,4,64,16,64]{5,2,4,3,0,1:T(4,128)} copy(f32[6,2,4,64,16,64]{5,4,0,1,3,2:T(8,128)} %bitcast.267) | data formatting | bytes 25165824 | tf_op jit(solution)/shard_map/all_to_all | solution.py:121
  1924.9 23.2 %all_to_all.67 = f32[6,2,64,16,256]{4,3,2,0,1:T(8,128)} reshape(f32[6,2,64,16,4,64]{5,4,3,2,0,1:T(4,128)} %bitcast.268) | data formatting | bytes 25165824 | tf_op jit(solution)/shard_map/all_to_all | solution.py:121
  (157 shorter events, 349.2 us)
Async XLA Ops:
  0.0 9.1 copy-start.17
  0.5 8.6 copy-start.22
  4.4 488.4 %copy-start.15 = (s32[256]{0:T(256)}, s32[256]{0:T(256)S(1)}, u32[]{:S(2)}) copy-start(s32[256]{0:T(256)S(1)} %get-tuple-element.6) | copy-start | bytes 3076
  5.0 4.2 copy-start.19
  462.8 12.9 copy-start.2
  462.8 19.8 slice-start.7
  475.7 6.9 slice-start.8
  585.5 324.3 %all-to-all-start.1 = ((f32[8,1,458752]{2,1,0:T(1,128)}), f32[8,1,458752]{2,1,0:T(1,128)}, u32[]{:S(2)}, u32[]{:S(2)}) async-start(f32[8,1,458752]{2,1,0:T(1,128)} %reshape.241), calls=%async_computation.1 | async-start | bytes 29360128 | tf_op jit(solution)/shard_map/all_to_all | solution.py:93
  1063.8 10.1 copy-start
  1539.8 10.8 copy-start.16
  1550.6 11.3 copy-start.4
  1582.1 11.5 copy-start.3
  1593.5 6.2 copy-start.6
  1599.8 6.9 copy-start.5
  1679.1 143.5 %all-to-all-start.3 = ((f32[4,1,786432]{2,1,0:T(1,128)}), f32[4,1,786432]{2,1,0:T(1,128)}, u32[]{:S(2)}, u32[]{:S(2)}) async-start(f32[4,1,786432]{2,1,0:T(1,128)} %reshape.245), calls=%async_computation.3 | async-start | bytes 25165824 | tf_op jit(solution)/shard_map/all_to_all | solution.py:121
  1685.4 23.5 %copy-start.24 = (f32[8]{0:T(128)S(1)}, f32[8]{0:T(128)}, u32[]{:S(2)}) copy-start(f32[8]{0:T(128)} %param.9) | copy-start | bytes 100
  1685.5 23.5 %copy-start.25 = (f32[8]{0:T(128)S(1)}, f32[8]{0:T(128)}, u32[]{:S(2)}) copy-start(f32[8]{0:T(128)} %param.8) | copy-start | bytes 100
  1685.5 23.7 %copy-start.21 = (s32[3]{0:T(128)S(1)}, s32[3]{0:T(128)}, u32[]{:S(2)}) copy-start(s32[3]{0:T(128)} %param.7) | copy-start | bytes 40
  1685.5 26.4 %copy-start.27 = (s32[64]{0:T(128)S(1)}, s32[64]{0:T(128)}, u32[]{:S(2)}) copy-start(s32[64]{0:T(128)} %get-tuple-element.12) | copy-start | bytes 772
  1685.5 26.5 %copy-start.26 = (f32[16]{0:T(128)S(1)}, f32[16]{0:T(128)}, u32[]{:S(2)}) copy-start(f32[16]{0:T(128)} %get-tuple-element.40) | copy-start | bytes 196
  1948.1 9.6 copy-start.1
  1979.6 8.9 copy-start.18
  1979.6 8.9 copy-start.20
  1979.6 8.9 copy-start.23
  1988.5 13.3 slice-start.2
  1992.1 9.8 slice-start.4
  1992.3 9.5 copy-start.11
  1992.3 9.5 copy-start.12
  1992.5 10.2 slice-start.3
  1992.5 11.4 slice-start.5
  1992.5 12.6 slice-start.6
  2012.8 4.1 copy-start.14
  (7 other events, 24.5 us)
where the time goes:
time: 2030 us; the launch traced here: 2020 us
  local copies, waits for them, and re-layouts  566 us (28%)
  blocking collectives  467 us (23%)
  waiting for transfers between devices  426 us (21%)
  other arithmetic  315 us (16%)
  matrix products  233 us (11%)
    all_to_all x1, waiting for transfers between devices, shards(): lax.all_to_all(grid_z, 'slab', split_axis=2, concat_axis=3, tiled=True)  319 us
    all_to_all x1, blocking collectives, shards(): lax.all_to_all(sectioned, 'slab', split_axis=3, concat_axis=2, tiled=True)  280 us
    unnamed x84, local copies, waits for them, and re-layouts  267 us
    all_to_all x1, blocking collectives, shards(): lax.all_to_all(spectral_y, 'grp', split_axis=4, concat_axis=2, tiled=True)  172 us
    all_to_all x1, waiting for transfers between devices, shards(): lax.all_to_all(spectral_z, 'grp', split_axis=2, concat_axis=4, tiled=True)  107 us
    unnamed x8, matrix products  78.6 us
    all_to_all x3, local copies, waits for them, and re-layouts, shards(): lax.all_to_all(spectral_y, 'grp', split_axis=4, concat_axis=2, tiled=True)  61.2 us
    all_to_all x2, local copies, waits for them, and re-layouts, shards(): lax.all_to_all(spectral_z, 'grp', split_axis=2, concat_axis=4, tiled=True)  53.4 us
  transfers between devices with their start and end apart: 2, of which 2 were waited for; matrix products, arithmetic and copies ran while one was open for 1% of the time, Pallas kernels for 0%

commit v1 on v0

v1 whole, which is shorter than its diff:
```python
import math

import jax
import jax.numpy as jnp
from jax import lax
from jax.sharding import PartitionSpec as P

PRECISE = lax.Precision.HIGH
TWO_PI = 6.283185307179586
TIME_STEP = 0.25
CORIOLIS = 1.0
BRUNT_SQUARED = 2.0
EPSILON = 1e-06


def signed(index, length):
    return jnp.where(index < length // 2, index, index - length)


def angles(modes, points, length):
    phase = modes[:, None] * points[None, :] % length
    theta = phase.astype(jnp.float32) * (TWO_PI / length)
    return (jnp.cos(theta), jnp.sin(theta))


def times_i(entries):
    return jnp.stack([-entries[1], entries[0]])


def mul(pattern, left, right):
    return jnp.einsum(pattern, left, right, precision=PRECISE)


def exchange(pieces, axis):
    shape = pieces.shape
    flat = pieces.reshape(shape[0], -1, shape[-2] * shape[-1])
    return lax.all_to_all(flat, axis, split_axis=0, concat_axis=0, tiled=True).reshape(shape)


def shards(state, kz_group, cutoffs, damping, power):
    grp_count = lax.axis_size("grp")
    slab_count = lax.axis_size("slab")
    grp_index = lax.axis_index("grp")
    slab_index = lax.axis_index("slab")
    slots_here = state.shape[2]
    cols_here = state.shape[3]
    NY = state.shape[4]
    NZ = slots_here * grp_count
    KX = cols_here * slab_count
    NX = 2 * KX
    GROUPS = damping.shape[0]
    GMODES = NZ // GROUPS
    rows_here = NY // grp_count
    planes_here = NZ // slab_count
    groups_here = GROUPS // grp_count
    normalizer = 1.0 / math.sqrt(NX * NY * NZ)
    slot_mode = jnp.argsort(kz_group, stable=True)
    local_mode = lax.dynamic_slice_in_dim(slot_mode, grp_index * slots_here, slots_here)
    mode_z = signed(local_mode, NZ)
    mode_x = slab_index * cols_here + jnp.arange(cols_here, dtype=jnp.int32)
    mode_y = signed(jnp.arange(NY, dtype=jnp.int32), NY)
    wave_z = (TWO_PI / NZ * mode_z.astype(jnp.float32))[:, None, None]
    wave_x = (TWO_PI / NX * mode_x.astype(jnp.float32))[None, :, None]
    wave_y = (TWO_PI / NY * mode_y.astype(jnp.float32))[None, None, :]
    flow_x, flow_y, flow_z, buoyant = (state[0], state[1], state[2], state[3])

    real_part = state[:, 0]
    imag_part = state[:, 1]
    cell_flux = real_part[2] * real_part[3] + imag_part[2] * imag_part[3]
    cell_energy = 0.5 * (
        jnp.sum(real_part[:3] ** 2 + imag_part[:3] ** 2, axis=0)
        + (real_part[3] ** 2 + imag_part[3] ** 2) / BRUNT_SQUARED
    )
    partial_value = jnp.stack(
        [jnp.sum(cell_flux, axis=(1, 2)), jnp.sum(cell_energy, axis=(1, 2))], axis=1
    )
    partial_value = jnp.sum(partial_value.reshape(groups_here, GMODES, 2), axis=1)
    totals = lax.psum(partial_value, "slab")
    means = totals / (GMODES * KX * NY)

    points_y = jnp.arange(NY, dtype=jnp.int32)
    points_z = jnp.arange(NZ, dtype=jnp.int32)
    points_x = jnp.arange(NX, dtype=jnp.int32)
    cosine_y, sine_y = angles(points_y, points_y, NY)
    from_real = jnp.stack([cosine_y, sine_y], axis=1)
    from_imag = jnp.stack([-sine_y, cosine_y], axis=1)
    column = wave_y.reshape(NY, 1, 1)
    shape_y = (NY, 2, grp_count, rows_here)
    spread = "fsxm,mdgy->gfdsxy"
    main = mul(spread, real_part, from_real.reshape(shape_y)) + mul(
        spread, imag_part, from_imag.reshape(shape_y)
    )
    slope = mul(spread, real_part[::2][:2], (column * from_imag).reshape(shape_y)) - mul(
        spread, imag_part[::2][:2], (column * from_real).reshape(shape_y)
    )
    pieces = exchange(jnp.concatenate([main, slope], axis=1), "grp")

    all_z = (TWO_PI / NZ * signed(slot_mode, NZ).astype(jnp.float32)).reshape(
        grp_count, slots_here, 1, 1
    )
    real_in, imag_in = (pieces[:, :, 0], pieces[:, :, 1])
    ru, rv, rw, rb, ruy, rwy = (real_in[:, k] for k in range(6))
    iu, iv, iw, ib, iuy, iwy = (imag_in[:, k] for k in range(6))
    reals = [ru, rv, rw, rb, rwy + all_z * iv, wave_x * iw - all_z * iu, -wave_x * iv - ruy]
    imags = [iu, iv, iw, ib, iwy - all_z * rv, all_z * ru - wave_x * rw, wave_x * rv - iuy]
    width = cols_here * rows_here
    reals = jnp.stack([r.reshape(NZ, width) for r in reals])
    imags = jnp.stack([r.reshape(NZ, width) for r in imags])
    cosine_z, sine_z = angles(slot_mode, points_z, NZ)
    shape_z = (NZ, 2, slab_count, planes_here)
    spread = "fsn,sdlz->lfdzn"
    grid_z = mul(spread, reals, jnp.stack([cosine_z, sine_z], axis=1).reshape(shape_z)) + mul(
        spread, imags, jnp.stack([-sine_z, cosine_z], axis=1).reshape(shape_z)
    )
    grid_z = grid_z.reshape(slab_count, 7, 2, planes_here, cols_here, rows_here)
    pieces = exchange(grid_z, "slab")

    weights = jnp.where(jnp.arange(KX) == 0, 1.0, 2.0).astype(jnp.float32) * normalizer
    cosine_x, sine_x = angles(jnp.arange(KX, dtype=jnp.int32), points_x, NX)
    shape_x = (2, slab_count, cols_here, NX)
    table_x = jnp.stack([cosine_x * weights[:, None], -sine_x * weights[:, None]]).reshape(shape_x)
    lines = pieces.transpose(1, 3, 5, 2, 0, 4).reshape(7, planes_here, rows_here, 2 * KX)
    grid = mul("fzyk,kn->fzyn", lines, table_x.reshape(2 * KX, NX))
    gu, gv, gw, gb, gox, goy, goz = (grid[k] for k in range(7))
    products = jnp.stack(
        [gv * goz - gw * goy, gw * gox - gu * goz, gu * goy - gv * gox, gu * gb, gv * gb, gw * gb]
    )
    table_b = jnp.stack([cosine_x * normalizer, -sine_x * normalizer]).reshape(2 * KX, NX)
    sectioned = mul("fzyn,kn->fzyk", products, table_b)
    sectioned = sectioned.reshape(6, planes_here, rows_here, 2, slab_count, cols_here)
    pieces = exchange(sectioned.transpose(4, 0, 3, 1, 5, 2), "slab")

    reals = pieces[:, :, 0].reshape(slab_count, 6, planes_here, width)
    imags = pieces[:, :, 1].reshape(slab_count, 6, planes_here, width)
    shape_z = (slab_count, planes_here, 2, grp_count, slots_here)
    cosine_z, sine_z = (cosine_z.T, sine_z.T)
    spread = "lfzn,lzdgs->dfgsn"
    back_z = mul(spread, reals, jnp.stack([cosine_z, -sine_z], axis=1).reshape(shape_z)) + mul(
        spread, imags, jnp.stack([sine_z, cosine_z], axis=1).reshape(shape_z)
    )
    back_z = back_z.reshape(2, 6, grp_count, slots_here, cols_here, rows_here)
    moved = wave_x * back_z[:, 3] + all_z * back_z[:, 5]
    chosen = [back_z[:, 0], back_z[:, 1], back_z[:, 2], moved, back_z[:, 4]]
    sent = jnp.stack([c.transpose(1, 0, 2, 3, 4) for c in chosen], axis=1)
    pieces = exchange(sent, "grp")

    lines = pieces.transpose(1, 2, 3, 4, 0, 5).reshape(5, 2, slots_here, cols_here, NY)
    table_r = jnp.stack([cosine_y, -sine_y], axis=1)
    table_i = jnp.stack([sine_y, cosine_y], axis=1)
    spread = "fsxy,ydm->fdsxm"
    tendency = mul(spread, lines[:, 0], table_r) + mul(spread, lines[:, 1], table_i)

    kept = (
        (96 * jnp.abs(mode_z) <= cutoffs[2] * NZ)[:, None, None]
        & (96 * mode_x <= cutoffs[0] * NX)[None, :, None]
        & (96 * jnp.abs(mode_y) <= cutoffs[1] * NY)[None, None, :]
    ).astype(jnp.float32)
    moment_x, moment_y, moment_z = (tendency[0] * kept, tendency[1] * kept, tendency[2] * kept)
    divergence = tendency[3] + wave_y * tendency[4]
    source_b = jnp.stack([divergence[1], -divergence[0]]) * kept
    power_here = lax.dynamic_slice_in_dim(power, grp_index * groups_here, groups_here)
    damping_here = lax.dynamic_slice_in_dim(damping, grp_index * groups_here, groups_here)
    forcing = (power_here - means[:, 0]) / (2.0 * (means[:, 1] + EPSILON))
    forcing_slot = jnp.repeat(forcing, GMODES)[:, None, None]
    damping_slot = jnp.repeat(damping_here, GMODES)[:, None, None]
    right_x = flow_x + TIME_STEP * (moment_x + forcing_slot * flow_x)
    right_y = flow_y + TIME_STEP * (moment_y + forcing_slot * flow_y)
    right_z = flow_z + TIME_STEP * (moment_z + forcing_slot * flow_z)
    right_b = buoyant + TIME_STEP * source_b
    wave_sq = wave_x * wave_x + wave_y * wave_y + wave_z * wave_z
    implicit = 1.0 + TIME_STEP * damping_slot * wave_sq
    rotation = TIME_STEP * CORIOLIS
    first_den = implicit * implicit + rotation * rotation
    second_den = implicit * implicit + TIME_STEP * TIME_STEP * BRUNT_SQUARED
    new_x = (implicit * right_x + rotation * right_y) / first_den
    new_y = (implicit * right_y - rotation * right_x) / first_den
    new_z = (implicit * right_z + TIME_STEP * right_b) / second_den
    new_b = (implicit * right_b - TIME_STEP * BRUNT_SQUARED * right_z) / second_den
    inverse_sq = 1.0 / (wave_sq + (wave_sq == 0).astype(jnp.float32))
    inner = (wave_x * new_x + wave_y * new_y + wave_z * new_z) * inverse_sq
    new_x = new_x - wave_x * inner
    new_y = new_y - wave_y * inner
    new_z = new_z - wave_z * inner
    return jnp.stack([new_x, new_y, new_z, new_b])


def solution(mesh):
    return jax.shard_map(
        shards,
        mesh=mesh,
        in_specs=(P(None, None, "grp", "slab", None), P(), P(), P(), P()),
        out_specs=P(None, None, "grp", "slab", None),
        check_vma=False,
    )
```

time: 2030 us -> 1540 us (0.76)
  blocking collectives: 467 us -> 14.5 us
  waiting for transfers between devices: 426 us -> 794 us
  other arithmetic: 315 us -> 87.9 us
  local copies, waits for them, and re-layouts: 566 us -> 461 us
  matrix products: 233 us -> 145 us
    all_to_all x2 -> x0, blocking collectives: 453 us -> none  [the longest x1 280 us: shards(): lax.all_to_all(sectioned, 'slab', split_axis=3, concat_axis=2, tiled=True)]
    all_to_all x2 -> x4, waiting for transfers between devices: 426 us -> 794 us  [exchange(): lax.all_to_all(flat, axis, split_axis=0, concat_axis=0, tiled=True)]
    unnamed x84 -> x105, local copies, waits for them, and re-layouts: 267 us -> 32.2 us
    reshape x0 -> x9, local copies, waits for them, and re-layouts: none -> 179 us  [the longest x4 78.4 us: exchange(): lax.all_to_all(flat, axis, split_axis=0, concat_axis=0, tiled=True)]
    all_to_all x4 -> x0, other arithmetic: 165 us -> none  [the longest x1 46.1 us: shards(): lax.all_to_all(spectral_y, 'grp', split_axis=4, concat_axis=2, tiled=True)]
    all_to_all x7 -> x0, local copies, waits for them, and re-layouts: 165 us -> none  [the longest x3 61.2 us: shards(): lax.all_to_all(spectral_y, 'grp', split_axis=4, concat_axis=2, tiled=True)]
    unnamed x8 -> x0, matrix products: 78.6 us -> none
    another operation x13 -> x4, other arithmetic: 79.6 us -> 3.09 us  [the longest x1 1.52 us: shards(): reals = jnp.stack([r.reshape(NZ, width) for r in reals])]
  transfers between devices with their start and end apart: 2 -> 4, of which waited for: 2 -> 4; matrix products, arithmetic and copies ran while one was open for 1% -> 2% of each run, Pallas kernels for 0% -> 0%
where the time goes in v1:
time: 1540 us; the launch traced here: 1530 us
  waiting for transfers between devices  794 us (52%)
  local copies, waits for them, and re-layouts  461 us (30%)
  matrix products  145 us (9%)
  other arithmetic  87.9 us (6%)
  starting transfers between devices  24.2 us (2%)
    all_to_all x4, waiting for transfers between devices, exchange(): lax.all_to_all(flat, axis, split_axis=0, concat_axis=0, tiled=True)  794 us
    dot_general x12, matrix products, mul(): return jnp.einsum(pattern, left, right, precision=PRECISE)  145 us
    reshape x4, local copies, waits for them, and re-layouts, exchange(): lax.all_to_all(flat, axis, split_axis=0, concat_axis=0, tiled=True)  78.4 us
    reshape x3, local copies, waits for them, and re-layouts, exchange(): flat = pieces.reshape(shape[0], -1, shape[-2] * shape[-1])  60.8 us
    unnamed x105, local copies, waits for them, and re-layouts  32.2 us
  transfers between devices with their start and end apart: 4, of which 4 were waited for; matrix products, arithmetic and copies ran while one was open for 2% of the time, Pallas kernels for 0%

profile of v1, /device:TPU:0, one launch (start us, length us, event | category | flops | bytes accessed | tf_op | source)
XLA Modules:
  0.0 1529.4 jit_solution(4487430191423126690)
XLA Ops:
  12.3 10.6 fusion.30
  23.0 15.6 %add_bitcast_fusion = f32[4,4,2,64,16,64]{3,5,4,1,0,2:T(8,128)} fusion(f32[2,4,64,4,64,16]{4,2,5,3,1,0:T(8,128)} %fusion.30, f32[4,1,64,16,256]{4,3,2,1,0:T(8,128)S(1)} %get-tuple-element.41, f32[256,1,4,64]{0,3,2,1:T(8,128)S(1)} %get-tuple-element.65, f32[256,1,4,64]{0,3,2,1:T(8,128)S(1)} %get-tuple-element.64), kind=kOutput, calls=%fused_computation.1 | convolution fusion | flops 3223453696 | bytes 21495808 | tf_op jit(solution)/shard_map/fsxm,mdgy->gfdsxy/dot_general | solution.py:31
  58.4 25.9 %copy.25 = f32[4,6,2,64,16,64]{5,4,3,2,1,0:T(8,128)} copy(f32[4,6,2,64,16,64]{3,5,4,1,0,2:T(8,128)} %pad_maximum_fusion) | data formatting | bytes 25165824 | tf_op jit(solution)/shard_map/concatenate | solution.py:96
  84.3 21.3 %reshape.1089 = f32[4,768,1024]{2,1,0:T(8,128)} reshape(f32[4,6,2,64,16,64]{5,4,3,2,1,0:T(8,128)} %copy.25) | data formatting | bytes 25165824 | tf_op jit(solution)/shard_map/reshape | solution.py:36
  118.9 132.3 %all-to-all-done = f32[4,768,1024]{2,1,0:T(8,128)} async-done(((f32[4,768,1024]{2,1,0:T(8,128)}), f32[4,768,1024]{2,1,0:T(8,128)}, u32[]{:S(2)}, u32[]{:S(2)}) %all-to-all-start) | async-done | bytes 12582944 | tf_op jit(solution)/shard_map/all_to_all | solution.py:37
  251.1 19.7 %reshape.1090 = f32[4,6,2,64,16,64]{5,4,3,2,1,0:T(8,128)} reshape(f32[4,768,1024]{2,1,0:T(8,128)} %all-to-all-done) | data formatting | bytes 25165824 | tf_op jit(solution)/shard_map/reshape | solution.py:37
  270.8 18.2 %slice_bitcast_fusion.1 = (f32[4,6,64,16,64]{4,3,2,1,0:T(8,128)}, f32[4,6,64,16,64]{4,3,2,1,0:T(8,128)}) fusion(f32[4,6,2,64,16,64]{5,4,3,2,1,0:T(8,128)} %reshape.1090), kind=kLoop, calls=%fused_computation.4 | loop fusion | bytes 25165824 | tf_op jit(solution)/shard_map/squeeze | solution.py:101
  352.8 13.5 fusion.6
  366.3 12.4 add_bitcast_fusion.1
  378.7 13.6 copy.26
  399.5 317.5 %all-to-all-done.1 = f32[8,448,1024]{2,1,0:T(8,128)} async-done(((f32[8,448,1024]{2,1,0:T(8,128)}), f32[8,448,1024]{2,1,0:T(8,128)}, u32[]{:S(2)}, u32[]{:S(2)}) %all-to-all-start.1) | async-done | bytes 14680096 | tf_op jit(solution)/shard_map/all_to_all | solution.py:37
  717.0 22.6 %reshape.1091 = f32[8,7,2,32,16,64]{5,4,3,2,1,0:T(8,128)} reshape(f32[8,448,1024]{2,1,0:T(8,128)} %all-to-all-done.1) | data formatting | bytes 29360128 | tf_op jit(solution)/shard_map/reshape | solution.py:37
  739.6 22.2 %copy.27 = f32[7,32,64,2,8,16]{2,5,4,3,1,0:T(8,128)} copy(f32[7,32,64,2,8,16]{2,5,1,3,0,4:T(8,128)} %bitcast.332) | data formatting | bytes 29360128 | tf_op jit(solution)/shard_map/transpose | solution.py:122
  761.7 31.3 %fusion.153 = f32[7,32,64,256]{3,2,1,0:T(8,128)} fusion(f32[7,32,64,256]{2,3,1,0:T(8,128)} %bitcast.331, f32[256,256,1,1]{1,0,3,2:T(8,128)S(1)} %bitcast.339), kind=kOutput, calls=%fused_computation.266 | convolution fusion | flops 5637144576 | bytes 29622272 | tf_op jit(solution)/shard_map/fzyk,kn->fzyn/dot_general | solution.py:31
  809.8 13.1 fusion.3
  832.0 21.3 %reshape.1093 = f32[8,384,1024]{2,1,0:T(8,128)} reshape(f32[8,6,2,32,16,64]{5,4,3,2,1,0:T(8,128)} %copy.29) | data formatting | bytes 25165824 | tf_op jit(solution)/shard_map/reshape | solution.py:36
  862.5 270.3 %all-to-all-done.2 = f32[8,384,1024]{2,1,0:T(8,128)} async-done(((f32[8,384,1024]{2,1,0:T(8,128)}), f32[8,384,1024]{2,1,0:T(8,128)}, u32[]{:S(2)}, u32[]{:S(2)}) %all-to-all-start.2) | async-done | bytes 12582944 | tf_op jit(solution)/shard_map/all_to_all | solution.py:37
  1132.8 19.7 %reshape.1094 = f32[8,6,2,32,16,64]{5,4,3,2,1,0:T(8,128)} reshape(f32[8,384,1024]{2,1,0:T(8,128)} %all-to-all-done.2) | data formatting | bytes 25165824 | tf_op jit(solution)/shard_map/reshape | solution.py:37
  1152.4 18.4 %fusion.147 = (f32[8,6,1,32,16,64]{5,4,3,2,1,0:T(8,128)}, f32[8,6,1,32,16,64]{5,4,3,2,1,0:T(8,128)}) fusion(f32[8,6,2,32,16,64]{5,4,3,2,1,0:T(8,128)} %reshape.1094), kind=kLoop, calls=%fused_computation.260 | loop fusion | bytes 25165824 | tf_op jit(solution)/shard_map/slice | solution.py:133
  1170.8 11.5 reshape.1125
  1182.4 11.6 reshape.1124
  1202.8 10.5 fusion
  1213.3 19.7 %reshape.1095 = f32[2,6,4,64,16,64]{5,4,3,1,2,0:T(8,128)} reshape(f32[2,6,4,64,1024]{4,3,1,2,0:T(8,128)} %fusion) | data formatting | bytes 25165824 | tf_op jit(solution)/shard_map/reshape | solution.py:141
  1233.0 16.4 %fusion.146 = (f32[2,1,4,64,16,64]{5,4,3,1,2,0:T(8,128)S(1)}, f32[2,1,4,64,16,64]{5,4,3,1,2,0:T(8,128)}, f32[2,1,4,64,16,64]{5,4,3,1,2,0:T(8,128)}, f32[2,1,4,64...) fusion(f32[2,6,4,64,16,64]{5,4,3,1,2,0:T(8,128)} %reshape.1095), kind=kLoop, calls=%fused_computation.259 | loop fusion | bytes 25165824 | tf_op jit(solution)/shard_map/slice | solution.py:143
  1268.2 18.2 %reshape.1096 = f32[4,640,1024]{2,1,0:T(8,128)} reshape(f32[4,5,2,64,16,64]{5,4,3,2,1,0:T(8,128)} %fusion.20) | data formatting | bytes 20971520 | tf_op jit(solution)/shard_map/reshape | solution.py:36
  1301.3 14.5 psum.7
  1333.7 73.5 %all-to-all-done.3 = f32[4,640,1024]{2,1,0:T(8,128)} async-done(((f32[4,640,1024]{2,1,0:T(8,128)}), f32[4,640,1024]{2,1,0:T(8,128)}, u32[]{:S(2)}, u32[]{:S(2)}) %all-to-all-start.3) | async-done | bytes 10485792 | tf_op jit(solution)/shard_map/all_to_all | solution.py:37
  1407.2 16.5 %reshape.1097 = f32[4,5,2,64,16,64]{5,4,3,2,1,0:T(8,128)} reshape(f32[4,640,1024]{2,1,0:T(8,128)} %all-to-all-done.3) | data formatting | bytes 20971520 | tf_op jit(solution)/shard_map/reshape | solution.py:37
  1423.7 25.5 %copy.38 = f32[5,2,64,16,4,64]{5,4,2,3,0,1:T(4,128)} copy(f32[5,2,64,16,4,64]{5,3,2,1,0,4:T(8,128)} %bitcast.333) | data formatting | bytes 20971520 | tf_op jit(solution)/shard_map/transpose | solution.py:147
  1449.2 19.8 %reshape.1098 = f32[5,2,64,16,256]{4,2,3,0,1:T(8,128)} reshape(f32[5,2,64,16,4,64]{5,4,2,3,0,1:T(4,128)} %copy.38) | data formatting | bytes 20971520 | tf_op jit(solution)/shard_map/reshape | solution.py:147
  1469.0 11.1 fusion.16
  1501.8 14.5 multiply_subtract_fusion.2
  (201 shorter events, 244.0 us)
Async XLA Ops:
  0.0 42.3 %copy-start.30 = (f32[256]{0:T(256)}, f32[256]{0:T(256)S(1)}, u32[]{:S(2)}) copy-start(f32[256]{0:T(256)S(1)} %convert_multiply_fusion) | copy-start | bytes 3076
  38.6 9.3 slice-start
  38.6 9.3 slice-start.1
  42.3 5.6 slice-start.2
  42.4 5.6 slice-start.3
  105.7 7.5 copy-start.39
  105.7 145.5 %all-to-all-start = ((f32[4,768,1024]{2,1,0:T(8,128)}), f32[4,768,1024]{2,1,0:T(8,128)}, u32[]{:S(2)}, u32[]{:S(2)}) async-start(f32[4,768,1024]{2,1,0:T(8,128)} %reshape.1089), calls=%async_computation | async-start | bytes 25165824 | tf_op jit(solution)/shard_map/all_to_all | solution.py:37
  116.3 154.5 %copy-start.34 = (s32[256]{0:T(256)}, s32[256]{0:T(256)S(1)}, u32[]{:S(2)}) copy-start(s32[256]{0:T(256)S(1)} %get-tuple-element.6) | copy-start | bytes 3076
  352.8 13.5 slice-start.4
  352.8 13.5 slice-start.5
  352.8 13.5 copy-start.27
  392.4 324.6 %all-to-all-start.1 = ((f32[8,448,1024]{2,1,0:T(8,128)}), f32[8,448,1024]{2,1,0:T(8,128)}, u32[]{:S(2)}, u32[]{:S(2)}) async-start(f32[8,448,1024]{2,1,0:T(8,128)} %bitcast.336), calls=%async_computation.1 | async-start | bytes 29360128 | tf_op jit(solution)/shard_map/all_to_all | solution.py:37
  793.1 10.1 copy-start
  853.3 5.7 copy-start.35
  853.3 5.9 copy-start.33
  853.3 279.5 %all-to-all-start.2 = ((f32[8,384,1024]{2,1,0:T(8,128)}), f32[8,384,1024]{2,1,0:T(8,128)}, u32[]{:S(2)}, u32[]{:S(2)}) async-start(f32[8,384,1024]{2,1,0:T(8,128)} %reshape.1093), calls=%async_computation.2 | async-start | bytes 25165824 | tf_op jit(solution)/shard_map/all_to_all | solution.py:37
  1194.0 8.8 copy-start.2
  1249.4 4.7 copy-start.9
  1257.8 5.0 copy-start.11
  1257.8 5.0 copy-start.37
  1286.4 120.8 %all-to-all-start.3 = ((f32[4,640,1024]{2,1,0:T(8,128)}), f32[4,640,1024]{2,1,0:T(8,128)}, u32[]{:S(2)}, u32[]{:S(2)}) async-start(f32[4,640,1024]{2,1,0:T(8,128)} %reshape.1096), calls=%async_computation.3 | async-start | bytes 20971520 | tf_op jit(solution)/shard_map/all_to_all | solution.py:37
  1296.2 19.6 %copy-start.40 = (f32[8]{0:T(128)S(1)}, f32[8]{0:T(128)}, u32[]{:S(2)}) copy-start(f32[8]{0:T(128)} %param.9) | copy-start | bytes 100
  1296.2 19.6 %copy-start.41 = (f32[8]{0:T(128)S(1)}, f32[8]{0:T(128)}, u32[]{:S(2)}) copy-start(f32[8]{0:T(128)} %param.8) | copy-start | bytes 100
  1296.2 19.9 %copy-start.38 = (s32[3]{0:T(128)S(1)}, s32[3]{0:T(128)}, u32[]{:S(2)}) copy-start(s32[3]{0:T(128)} %param.7) | copy-start | bytes 40
  1469.0 11.1 copy-start.1
  1469.0 11.1 copy-start.26
  1469.0 11.1 copy-start.29
  1480.1 8.9 copy-start.31
  1480.2 9.5 copy-start.14
  1480.2 9.5 copy-start.15
  1489.6 12.2 copy-start.17
  1489.6 12.2 copy-start.18
  (20 other events, 63.3 us)
